TPU v7x, 32 devices: a whole 2x2x4 slice. The times are simulated.
32 devices in a mesh: tilt: 2 (over y), row: 8 (over z, x), col: 2 (over core).
Axes of the slice: x: 2, y: 2, z: 4, core: 2. Of those that a mesh axis runs over, the one named last changes fastest.
Arguments:
- object_field: float32 [2, 2048, 256], P(None, ('tilt', 'row'), 'col'), parts along dimension 1, may hold values from -4.2 to 4.2
- probe: float32 [8, 2, 128, 128], P('tilt'), parts along dimension 0, may hold values from -2.1 to 2.1
- patterns: float32 [16, 2, 2, 128, 128], P(('tilt', 'row'), 'col'), parts along dimension 0, may hold values from 0.1 to 3
- offsets: int32 [16, 2, 2, 2], P(('tilt', 'row'), 'col'), parts along dimension 0, may hold values from 0 to 256
- counts: int32 [16, 2], P(('tilt', 'row'), 'col'), parts along dimension 0, may hold values from 1 to 2, as said below
Outputs:
- object_out: float32 [2, 2048, 256], P(None, ('tilt', 'row'), 'col'), parts along dimension 1
- probe_out: float32 [8, 2, 128, 128], P('tilt'), parts along dimension 0
There are 2 independent parts, one for each index of `tilt`. A program takes and returns all parts, laid end to end along the dimension named above; each array names one. Nothing has to cross between parts.
Inputs may be any that keep to these rules, and one draw needn't show every extreme that they name: Only the first counts[r, c] slots of a tile are live; some tile has all 2 live. `offsets`: A window lies inside its tile's frame of 384 pixels a side.
All inputs are finite; a program needn't handle non-finite values.
Results may differ from a plain program's by a relative error of at most 0.0003.
Values sent between devices are 32-bit elements; how exact they have to be, the bound alone decides.
A program may use at most 64 MiB of HBM per device.

v0:
```python
import jax
import jax.numpy as jnp
from jax import lax
from jax.sharding import PartitionSpec as P

H = 128
object_rate = 1.0
probe_rate = 1.0
epsilon = 1e-06


def with_halo(block, sides, width):
    for axis, dim in sides:
        count = lax.axis_size(axis)
        forward = [(i, i + 1) for i in range(count - 1)]
        backward = [(target, source) for source, target in forward]
        low = lax.ppermute(
            lax.slice_in_dim(block, block.shape[dim] - width, None, axis=dim), axis, forward
        )
        high = lax.ppermute(lax.slice_in_dim(block, 0, width, axis=dim), axis, backward)
        block = jnp.concatenate([low, block, high], axis=dim)
    return block


def as_index(value):
    return jnp.asarray(value).astype(jnp.int32)


def dft_tables(length):
    counter = jnp.arange(length, dtype=jnp.int32)
    product = counter[:, None] * counter[None, :] % length
    angle = -2.0 * jnp.pi / length * product.astype(jnp.float32)
    norm = 1.0 / jnp.sqrt(jnp.float32(length))
    return (jnp.cos(angle) * norm, jnp.sin(angle) * norm)


def left_product(cos_table, sin_table, real_part, imag_part):
    hp = lax.Precision.HIGHEST
    real_out = jnp.einsum("ab,kbc->kac", cos_table, real_part, precision=hp) - jnp.einsum(
        "ab,kbc->kac", sin_table, imag_part, precision=hp
    )
    imag_out = jnp.einsum("ab,kbc->kac", cos_table, imag_part, precision=hp) + jnp.einsum(
        "ab,kbc->kac", sin_table, real_part, precision=hp
    )
    return (real_out, imag_out)


def right_product(real_part, imag_part, cos_table, sin_table):
    hp = lax.Precision.HIGHEST
    real_out = jnp.einsum("kab,bc->kac", real_part, cos_table, precision=hp) - jnp.einsum(
        "kab,bc->kac", imag_part, sin_table, precision=hp
    )
    imag_out = jnp.einsum("kab,bc->kac", real_part, sin_table, precision=hp) + jnp.einsum(
        "kab,bc->kac", imag_part, cos_table, precision=hp
    )
    return (real_out, imag_out)


def transform(real_part, imag_part, cos_table, sin_table):
    middle_re, middle_im = left_product(cos_table, sin_table, real_part, imag_part)
    return right_product(middle_re, middle_im, cos_table, sin_table)


def slot_terms(window, probe, pattern, cos_table, sin_table):
    window_re, window_im = (window[0], window[1])
    probe_re, probe_im = (probe[:, 0], probe[:, 1])
    exit_re = probe_re * window_re - probe_im * window_im
    exit_im = probe_re * window_im + probe_im * window_re
    far_re, far_im = transform(exit_re, exit_im, cos_table, sin_table)
    intensity = jnp.sum(far_re * far_re + far_im * far_im, axis=0)
    misfit = intensity - pattern
    back_re, back_im = transform(misfit * far_re, misfit * far_im, cos_table, -sin_table)
    grad_re = jnp.sum(probe_re * back_re + probe_im * back_im, axis=0)
    grad_im = jnp.sum(probe_re * back_im - probe_im * back_re, axis=0)
    term_re = window_re * back_re + window_im * back_im
    term_im = window_re * back_im - window_im * back_re
    return (jnp.stack([grad_re, grad_im]), jnp.stack([term_re, term_im], axis=1))


def body(object_field, probe, patterns, offsets, counts):
    width = probe.shape[-1]
    block = object_field.shape[1]
    slot_total = patterns.shape[2]
    cos_table, sin_table = dft_tables(width)
    tile_total = lax.axis_size("row") * lax.axis_size("col")
    live_count = counts[0, 0]
    frame = with_halo(object_field, (("row", 1), ("col", 2)), H)

    def slot_step(slot_index, inner):
        local_grad, probe_acc = inner
        slot_index = as_index(slot_index)
        corner_y = as_index(offsets[0, 0, slot_index, 0])
        corner_x = as_index(offsets[0, 0, slot_index, 1])
        window = lax.dynamic_slice(frame, (as_index(0), corner_y, corner_x), (2, width, width))
        window_grad, probe_term = slot_terms(
            window, probe, patterns[0, 0, slot_index], cos_table, sin_table
        )
        live = (slot_index < live_count).astype(jnp.float32)
        region = (
            lax.dynamic_slice(local_grad, (as_index(0), corner_y, corner_x), (2, width, width))
            + live * window_grad
        )
        local_grad = lax.dynamic_update_slice(local_grad, region, (as_index(0), corner_y, corner_x))
        return (local_grad, probe_acc + live * probe_term)

    start_carry = (jnp.zeros_like(frame), jnp.zeros_like(probe))
    gradient, probe_grad = lax.fori_loop(0, slot_total, slot_step, start_carry)
    upper_strip = gradient[:, :H, :]
    lower_strip = gradient[:, H + block :, :]
    middle = gradient[:, H : H + block, :]
    row_edges = jnp.concatenate([upper_strip, lower_strip], axis=1)
    row_grown = with_halo(row_edges, (("row", 1),), H)
    from_above = row_grown[:, :H, :]
    from_below = row_grown[:, 3 * H :, :]
    middle = middle.at[:, :H, :].add(from_above).at[:, block - H :, :].add(from_below)
    left_strip = middle[:, :, :H]
    right_strip = middle[:, :, H + block :]
    object_grad = middle[:, :, H : H + block]
    col_edges = jnp.concatenate([left_strip, right_strip], axis=2)
    col_grown = with_halo(col_edges, (("col", 2),), H)
    from_left = col_grown[:, :, :H]
    from_right = col_grown[:, :, 3 * H :]
    object_grad = object_grad.at[:, :, :H].add(from_left).at[:, :, block - H :].add(from_right)
    weight = (
        jnp.max(jnp.sum(probe[:, 0] * probe[:, 0] + probe[:, 1] * probe[:, 1], axis=0)) + epsilon
    )
    object_field = object_field - object_rate * object_grad / weight
    summed = lax.psum(probe_grad, ("row", "col"))
    probe = probe - probe_rate * summed / tile_total
    return (object_field, probe)


def solution(mesh):
    placed = (
        P(None, ("tilt", "row"), "col"),
        P("tilt", None, None, None),
        P(("tilt", "row"), "col", None, None, None),
        P(("tilt", "row"), "col", None, None),
        P(("tilt", "row"), "col"),
    )
    return jax.shard_map(
        body,
        mesh=mesh,
        in_specs=placed,
        out_specs=(P(None, ("tilt", "row"), "col"), P("tilt", None, None, None)),
        check_vma=False,
    )
```

profile of v0, /device:TPU:0, one launch (start us, length us, event | category | flops | bytes accessed | tf_op | source)
XLA Modules:
  0.0 179.6 jit_solution(4061278362378386647)
XLA Ops:
  7.2 4.9 %collective-permute-start = (f32[2,128,128]{2,1,0:T(8,128)}, f32[2,128,128]{2,1,0:T(8,128)S(1)}, u32[]{:S(2)}, u32[]{:S(2)}) collective-permute-start(f32[2,128,128]{2,1,0:T(8,128)} %param.23), channel_id=1, source_target_pairs={{0,2},{2,4},{4,6},{6,8},{8,10},{10,12},{12,14},{1,3},{3,5},{5,7},{... | collective-permute-start | bytes 393224 | tf_op jit(solution)/shard_map/ppermute | solution.py:17
  12.1 1.3 collective-permute-start.1
  13.4 1.7 collective-permute-done
  15.2 0.9 constant_dynamic-update-slice_fusion.1
  16.1 3.1 %collective-permute-done.1 = f32[2,128,128]{2,1,0:T(8,128)S(1)} collective-permute-done((f32[2,128,128]{2,1,0:T(8,128)}, f32[2,128,128]{2,1,0:T(8,128)S(1)}, u32[]{:S(2)}, u32[]{:S(2)}) %collective-permute-start.1) | collective-permute-done | bytes 131104 | tf_op jit(solution)/shard_map/ppermute | solution.py:20
  19.2 1.3 collective-permute-start.2
  20.5 1.3 collective-permute-start.3
  21.8 1.1 copy.41
  22.9 1.2 collective-permute-done.3
  24.1 1.1 pad_maximum_fusion
  25.3 0.8 copy-done.1
  26.1 42.0 %while.26 = (s32[]{:T(128)}, f32[2,384,384]{2,1,0:T(8,128)S(1)}, f32[4,2,128,128]{3,2,0,1:T(8,128)S(1)}, s32[1,1,2,2]{3,2,1,0:T(2,128)S(1)}, s32[]{:T(128)}, /*i...) while((s32[]{:T(128)}, f32[2,384,384]{2,1,0:T(8,128)S(1)}, ...), condition=%wide.region_4.5_spmd.clone.clone, body=%wide.region_0.4_spmd.clone.clone.sunk | while | flops 1617952768 | bytes 16646421 | solution.py:107
  30.7 1.1 dynamic-slice_bitcast_fusion.3
  44.8 2.2 %dynamic_update_slice.11 = f32[2,384,384]{2,1,0:T(8,128)S(1)} dynamic-update-slice(f32[2,384,384]{2,1,0:T(8,128)S(1)} %get-tuple-element.543, f32[2,128,128]{2,1,0:T(8,128)S(1)} %fusion.247, s32[]{:T(128)} %constant.191.clone.1..sunk, s32[]{:T(128)S(6)} %select_n.177, s32[]{:T(128)S(6)} %select_n.178) | dynamic-update-slice | bytes 262148 | tf_op jit(solution)/shard_map/while/body/eval_jaxpr/dynamic_update_slice | solution.py:103
  51.6 1.1 dynamic-slice_bitcast_fusion.3
  65.6 2.5 %dynamic_update_slice.11 = f32[2,384,384]{2,1,0:T(8,128)S(1)} dynamic-update-slice(f32[2,384,384]{2,1,0:T(8,128)S(1)} %get-tuple-element.543, f32[2,128,128]{2,1,0:T(8,128)S(1)} %fusion.247, s32[]{:T(128)} %constant.191.clone.1..sunk, s32[]{:T(128)S(6)} %select_n.177, s32[]{:T(128)S(6)} %select_n.178) | dynamic-update-slice | bytes 262148 | tf_op jit(solution)/shard_map/while/body/eval_jaxpr/dynamic_update_slice | solution.py:103
  69.0 4.5 %collective-permute-start.4 = (f32[2,128,384]{2,1,0:T(8,128)}, f32[2,128,384]{2,1,0:T(8,128)S(1)}, u32[]{:S(2)}, u32[]{:S(2)}) collective-permute-start(f32[2,128,384]{2,1,0:T(8,128)} %get-tuple-element.457), channel_id=1, source_target_pairs={{0,2},{2,4},{4,6},{6,8},{8,10},{10,12},{12,14},{1,3},{3,5},{5,7},{... | collective-permute-start | bytes 1179656 | tf_op jit(solution)/shard_map/ppermute | solution.py:17
  73.5 1.3 collective-permute-start.5
  76.1 0.8 copy.42
  77.0 14.1 %collective-permute-done.4 = f32[2,128,384]{2,1,0:T(8,128)S(1)} collective-permute-done((f32[2,128,384]{2,1,0:T(8,128)}, f32[2,128,384]{2,1,0:T(8,128)S(1)}, u32[]{:S(2)}, u32[]{:S(2)}) %collective-permute-start.4) | collective-permute-done | bytes 393248 | tf_op jit(solution)/shard_map/ppermute | solution.py:17
  91.1 1.4 collective-permute-start.6
  92.6 1.3 collective-permute-start.7
  93.9 76.3 %all-reduce.2.cloned.1.call-done = f32[4,2,128,128]{3,2,1,0:T(8,128)} async-done(((f32[4,2,128,128]{3,2,1,0:T(8,128)}), f32[4,2,128,128]{3,2,1,0:T(8,128)}) %all-reduce.2.cloned.1.call-update) | async-done | bytes 524304 | tf_op jit(solution)/shard_map/psum | solution.py:128
  170.2 1.9 %multiply_subtract_fusion = f32[4,2,128,128]{3,2,1,0:T(8,128)} fusion(f32[4,2,128,128]{3,2,1,0:T(8,128)S(1)} %copy-done, f32[4,2,128,128]{3,2,1,0:T(8,128)} %all-reduce.2.cloned.1.call-done), kind=kLoop, calls=%fused_computation.169 | loop fusion | flops 262144 | bytes 1572864 | tf_op jit(solution)/shard_map/sub | solution.py:129
  (63 shorter events, 28.0 us)
Async XLA Ops:
  7.2 163.0 %all-reduce.2.cloned.1.call-start = ((), (), s32[]{:S(2)}) async-start(), calls=%async_computation | async-start | bytes 1048576 | tf_op jit(solution)/shard_map/psum | solution.py:128
  7.2 7.9 %collective-permute-start = (f32[2,128,128]{2,1,0:T(8,128)}, f32[2,128,128]{2,1,0:T(8,128)S(1)}, u32[]{:S(2)}, u32[]{:S(2)}) collective-permute-start(f32[2,128,128]{2,1,0:T(8,128)} %param.23), channel_id=1, source_target_pairs={{0,2},{2,4},{4,6},{6,8},{8,10},{10,12},{12,14},{1,3},{3,5},{5,7},{... | collective-permute-start | bytes 393224 | tf_op jit(solution)/shard_map/ppermute | solution.py:17
  12.1 7.1 %collective-permute-start.1 = (f32[2,128,128]{2,1,0:T(8,128)}, f32[2,128,128]{2,1,0:T(8,128)S(1)}, u32[]{:S(2)}, u32[]{:S(2)}) collective-permute-start(f32[2,128,128]{2,1,0:T(8,128)} %param.23), channel_id=1, source_target_pairs={{2,0},{4,2},{6,4},{8,6},{10,8},{12,10},{14,12},{3,1},{5,3},{7,5},{... | collective-permute-start | bytes 393224 | tf_op jit(solution)/shard_map/ppermute | solution.py:20
  19.2 3.7 %collective-permute-start.2 = (f32[2,384,128]{2,1,0:T(8,128)S(1)}, f32[2,384,128]{2,1,0:T(8,128)S(1)}, u32[]{:S(2)}, u32[]{:S(2)}) collective-permute-start(f32[2,384,128]{2,1,0:T(8,128)S(1)} %constant_dynamic-update-slice_fusion), channel_id=1, source_target_pairs={{0,1},{2,3},{4,5},{6,7},{8,9},{10,11},{12,13},{14,15},{16,17},{18,... | collective-permute-start | bytes 1179656 | tf_op jit(solution)/shard_map/ppermute | solution.py:17
  20.5 3.6 %collective-permute-start.3 = (f32[2,384,128]{2,1,0:T(8,128)S(1)}, f32[2,384,128]{2,1,0:T(8,128)S(1)}, u32[]{:S(2)}, u32[]{:S(2)}) collective-permute-start(f32[2,384,128]{2,1,0:T(8,128)S(1)} %constant_dynamic-update-slice_fusion), channel_id=1, source_target_pairs={{1,0},{3,2},{5,4},{7,6},{9,8},{11,10},{13,12},{15,14},{17,16},{19,... | collective-permute-start | bytes 1179656 | tf_op jit(solution)/shard_map/ppermute | solution.py:20
  25.2 0.9 copy-start.1
  25.2 0.9 copy-start.3
  68.2 6.6 %copy-start = (f32[4,2,128,128]{3,2,1,0:T(8,128)S(1)}, f32[4,2,128,128]{3,2,1,0:T(8,128)}, u32[]{:S(2)}) copy-start(f32[4,2,128,128]{3,2,1,0:T(8,128)} %param.24) | copy-start | bytes 1572868
  69.0 22.0 %collective-permute-start.4 = (f32[2,128,384]{2,1,0:T(8,128)}, f32[2,128,384]{2,1,0:T(8,128)S(1)}, u32[]{:S(2)}, u32[]{:S(2)}) collective-permute-start(f32[2,128,384]{2,1,0:T(8,128)} %get-tuple-element.457), channel_id=1, source_target_pairs={{0,2},{2,4},{4,6},{6,8},{8,10},{10,12},{12,14},{1,3},{3,5},{5,7},{... | collective-permute-start | bytes 1179656 | tf_op jit(solution)/shard_map/ppermute | solution.py:17
  73.5 17.5 %collective-permute-start.5 = (f32[2,128,384]{2,1,0:T(8,128)S(1)}, f32[2,128,384]{2,1,0:T(8,128)S(1)}, u32[]{:S(2)}, u32[]{:S(2)}) collective-permute-start(f32[2,128,384]{2,1,0:T(8,128)S(1)} %get-tuple-element.458), channel_id=1, source_target_pairs={{2,0},{4,2},{6,4},{8,6},{10,8},{12,10},{14,12},{3,1},{5,3},{7,5},{... | collective-permute-start | bytes 1179656 | tf_op jit(solution)/shard_map/ppermute | solution.py:20
  91.1 81.0 %copy-start.2 = (f32[2,128,128]{2,1,0:T(8,128)S(1)}, f32[2,128,128]{2,1,0:T(8,128)}, u32[]{:S(2)}) copy-start(f32[2,128,128]{2,1,0:T(8,128)} %param.23) | copy-start | bytes 393220
  91.1 81.0 %collective-permute-start.6 = (f32[2,128,128]{2,1,0:T(8,128)S(1)}, f32[2,128,128]{2,1,0:T(8,128)S(1)}, u32[]{:S(2)}, u32[]{:S(2)}) collective-permute-start(f32[2,128,128]{2,1,0:T(8,128)S(1)} %get-tuple-element.459), channel_id=1, source_target_pairs={{0,1},{2,3},{4,5},{6,7},{8,9},{10,11},{12,13},{14,15},{16,17},{18,... | collective-permute-start | bytes 393224 | tf_op jit(solution)/shard_map/ppermute | solution.py:17
  92.6 79.5 %collective-permute-start.7 = (f32[2,128,128]{2,1,0:T(8,128)S(1)}, f32[2,128,128]{2,1,0:T(8,128)S(1)}, u32[]{:S(2)}, u32[]{:S(2)}) collective-permute-start(f32[2,128,128]{2,1,0:T(8,128)S(1)} %get-tuple-element.460), channel_id=1, source_target_pairs={{1,0},{3,2},{5,4},{7,6},{9,8},{11,10},{13,12},{15,14},{17,16},{19,... | collective-permute-start | bytes 393224 | tf_op jit(solution)/shard_map/ppermute | solution.py:20
Sparse Core Ops, SparseCore 0:
  77.1 93.0 all-reduce.1
where the time goes:
time: 180 us
  waiting for transfers between devices  96.5 us (54%)
  matrix products  23.8 us (13%)
  starting transfers between devices  17.3 us (10%)
  between operations  14.8 us (8%)
  local copies, waits for them, and re-layouts  12.6 us (7%)
  loops' own time  9.63 us (5%)
  other arithmetic  4.97 us (3%)
    psum x1, waiting for transfers between devices, body(): summed = lax.psum(probe_grad, ('row', 'col'))  76.3 us
    ppermute x4, waiting for transfers between devices, with_halo(): lax.ppermute(lax.slice_in_dim(block, block.shape[dim] - width, None, axis...  15.8 us
    ppermute x4, starting transfers between devices, with_halo(): lax.ppermute(lax.slice_in_dim(block, block.shape[dim] - width, None, axis...  12.1 us
    another operation x1, loops' own time, body(): gradient, probe_grad = lax.fori_loop(0, slot_total, slot_step, start_carry)  9.63 us
    ppermute x4, starting transfers between devices, with_halo(): lax.ppermute(lax.slice_in_dim(block, 0, width, axis=dim), axis, backward)  5.17 us
    dynamic_update_slice x2, local copies, waits for them, and re-layouts, slot_step(): lax.dynamic_update_slice(local_grad, region, (as_index(0), corner_y, corn...  4.66 us
    ppermute x4, waiting for transfers between devices, with_halo(): lax.ppermute(lax.slice_in_dim(block, 0, width, axis=dim), axis, backward)  4.31 us
  transfers between devices with their start and end apart: 9, of which 5 were waited for; matrix products, arithmetic and copies ran while one was open for 3% of the time, Pallas kernels for 0%

commit v1 on v0

--- a/solution.py
+++ b/solution.py
@@ -125,7 +125,7 @@
         jnp.max(jnp.sum(probe[:, 0] * probe[:, 0] + probe[:, 1] * probe[:, 1], axis=0)) + epsilon
     )
     object_field = object_field - object_rate * object_grad / weight
-    summed = lax.psum(probe_grad, ("row", "col"))
+    summed = lax.psum(lax.psum(probe_grad, "col"), "row")
     probe = probe - probe_rate * summed / tile_total
     return (object_field, probe)
 

time: 180 us -> 182 us (1.011)
  waiting for transfers between devices: 96.5 us -> 98.4 us
    psum x1 -> x2, waiting for transfers between devices: 76.3 us -> 77.6 us  [body(): summed = lax.psum(lax.psum(probe_grad, 'col'), 'row')]
  transfers between devices with their start and end apart: 9 -> 10, of which waited for: 5 -> 7; matrix products, arithmetic and copies ran while one was open for 3% -> 2% of each run, Pallas kernels for 0% -> 0%
where the time goes in v1:
time: 182 us
  waiting for transfers between devices  98.4 us (54%)
  matrix products  23.8 us (13%)
  starting transfers between devices  18.1 us (10%)
  between operations  14.9 us (8%)
  local copies, waits for them, and re-layouts  11.9 us (7%)
  loops' own time  9.63 us (5%)
  other arithmetic  4.96 us (3%)
    psum x2, waiting for transfers between devices, body(): summed = lax.psum(lax.psum(probe_grad, 'col'), 'row')  77.6 us
    ppermute x4, waiting for transfers between devices, with_halo(): lax.ppermute(lax.slice_in_dim(block, block.shape[dim] - width, None, axis...  15.8 us
    ppermute x4, starting transfers between devices, with_halo(): lax.ppermute(lax.slice_in_dim(block, block.shape[dim] - width, None, axis...  12.9 us
    another operation x1, loops' own time, body(): gradient, probe_grad = lax.fori_loop(0, slot_total, slot_step, start_carry)  9.63 us
    ppermute x4, starting transfers between devices, with_halo(): lax.ppermute(lax.slice_in_dim(block, 0, width, axis=dim), axis, backward)  5.17 us
    ppermute x4, waiting for transfers between devices, with_halo(): lax.ppermute(lax.slice_in_dim(block, 0, width, axis=dim), axis, backward)  4.92 us
    dynamic_update_slice x2, local copies, waits for them, and re-layouts, slot_step(): lax.dynamic_update_slice(local_grad, region, (as_index(0), corner_y, corn...  4.66 us
  transfers between devices with their start and end apart: 10, of which 7 were waited for; matrix products, arithmetic and copies ran while one was open for 2% of the time, Pallas kernels for 0%

profile of v1, /device:TPU:0, one launch (start us, length us, event | category | flops | bytes accessed | tf_op | source)
XLA Modules:
  0.0 181.6 jit_solution(8756795640430662466)
XLA Ops:
  7.2 4.9 %collective-permute-start = (f32[2,128,128]{2,1,0:T(8,128)}, f32[2,128,128]{2,1,0:T(8,128)S(1)}, u32[]{:S(2)}, u32[]{:S(2)}) collective-permute-start(f32[2,128,128]{2,1,0:T(8,128)} %param.23), channel_id=1, source_target_pairs={{0,2},{2,4},{4,6},{6,8},{8,10},{10,12},{12,14},{1,3},{3,5},{5,7},{... | collective-permute-start | bytes 393224 | tf_op jit(solution)/shard_map/ppermute | solution.py:17
  12.1 1.3 collective-permute-start.1
  13.4 1.7 collective-permute-done
  15.2 0.9 constant_dynamic-update-slice_fusion.1
  16.1 3.1 %collective-permute-done.1 = f32[2,128,128]{2,1,0:T(8,128)S(1)} collective-permute-done((f32[2,128,128]{2,1,0:T(8,128)}, f32[2,128,128]{2,1,0:T(8,128)S(1)}, u32[]{:S(2)}, u32[]{:S(2)}) %collective-permute-start.1) | collective-permute-done | bytes 131104 | tf_op jit(solution)/shard_map/ppermute | solution.py:20
  19.2 1.3 collective-permute-start.2
  20.5 1.3 collective-permute-start.3
  21.8 1.1 copy.41
  22.9 1.2 collective-permute-done.3
  24.1 1.1 pad_maximum_fusion
  26.1 42.0 %while.26 = (s32[]{:T(128)}, f32[2,384,384]{2,1,0:T(8,128)S(1)}, f32[4,2,128,128]{3,2,0,1:T(8,128)S(1)}, s32[1,1,2,2]{3,2,1,0:T(2,128)S(1)}, s32[]{:T(128)}, /*i...) while((s32[]{:T(128)}, f32[2,384,384]{2,1,0:T(8,128)S(1)}, ...), condition=%wide.region_4.5_spmd.clone.clone, body=%wide.region_0.4_spmd.clone.clone.sunk | while | flops 1617952768 | bytes 16646421 | solution.py:107
  30.7 1.1 dynamic-slice_bitcast_fusion.3
  44.8 2.2 %dynamic_update_slice.11 = f32[2,384,384]{2,1,0:T(8,128)S(1)} dynamic-update-slice(f32[2,384,384]{2,1,0:T(8,128)S(1)} %get-tuple-element.543, f32[2,128,128]{2,1,0:T(8,128)S(1)} %fusion.247, s32[]{:T(128)} %constant.191.clone.1..sunk, s32[]{:T(128)S(6)} %select_n.177, s32[]{:T(128)S(6)} %select_n.178) | dynamic-update-slice | bytes 262148 | tf_op jit(solution)/shard_map/while/body/eval_jaxpr/dynamic_update_slice | solution.py:103
  51.6 1.1 dynamic-slice_bitcast_fusion.3
  65.6 2.5 %dynamic_update_slice.11 = f32[2,384,384]{2,1,0:T(8,128)S(1)} dynamic-update-slice(f32[2,384,384]{2,1,0:T(8,128)S(1)} %get-tuple-element.543, f32[2,128,128]{2,1,0:T(8,128)S(1)} %fusion.247, s32[]{:T(128)} %constant.191.clone.1..sunk, s32[]{:T(128)S(6)} %select_n.177, s32[]{:T(128)S(6)} %select_n.178) | dynamic-update-slice | bytes 262148 | tf_op jit(solution)/shard_map/while/body/eval_jaxpr/dynamic_update_slice | solution.py:103
  68.2 4.5 %collective-permute-start.4 = (f32[2,128,384]{2,1,0:T(8,128)S(1)}, f32[2,128,384]{2,1,0:T(8,128)S(1)}, u32[]{:S(2)}, u32[]{:S(2)}) collective-permute-start(f32[2,128,384]{2,1,0:T(8,128)S(1)} %get-tuple-element.457), channel_id=1, source_target_pairs={{0,2},{2,4},{4,6},{6,8},{8,10},{10,12},{12,14},{1,3},{3,5},{5,7},{... | collective-permute-start | bytes 1179656 | tf_op jit(solution)/shard_map/ppermute | solution.py:17
  72.8 1.3 collective-permute-start.5
  74.1 0.8 copy.42
  75.0 14.1 %collective-permute-done.4 = f32[2,128,384]{2,1,0:T(8,128)S(1)} collective-permute-done((f32[2,128,384]{2,1,0:T(8,128)S(1)}, f32[2,128,384]{2,1,0:T(8,128)S(1)}, u32[]{:S(2)}, u32[]{:S(2)}) %collective-permute-start.4) | collective-permute-done | bytes 393248 | tf_op jit(solution)/shard_map/ppermute | solution.py:17
  89.1 6.4 %all-reduce.3.cloned.1.call-done = f32[4,2,128,128]{3,2,1,0:T(8,128)} async-done(((f32[4,2,128,128]{3,2,1,0:T(8,128)}), f32[4,2,128,128]{3,2,1,0:T(8,128)}) %all-reduce.3.cloned.1.call-update) | async-done | bytes 524304 | tf_op jit(solution)/shard_map/psum | solution.py:128
  95.6 2.2 %collective-permute-start.6 = (f32[2,128,128]{2,1,0:T(8,128)S(1)}, f32[2,128,128]{2,1,0:T(8,128)S(1)}, u32[]{:S(2)}, u32[]{:S(2)}) collective-permute-start(f32[2,128,128]{2,1,0:T(8,128)S(1)} %get-tuple-element.459), channel_id=1, source_target_pairs={{0,1},{2,3},{4,5},{6,7},{8,9},{10,11},{12,13},{14,15},{16,17},{18,... | collective-permute-start | bytes 393224 | tf_op jit(solution)/shard_map/ppermute | solution.py:17
  97.8 1.3 collective-permute-start.7
  101.7 71.2 %all-reduce.5.cloned.1.call-done = f32[4,2,128,128]{3,2,1,0:T(8,128)} async-done(((f32[4,2,128,128]{3,2,1,0:T(8,128)}), f32[4,2,128,128]{3,2,1,0:T(8,128)}) %all-reduce.5.cloned.1.call-update) | async-done | bytes 524304 | tf_op jit(solution)/shard_map/psum | solution.py:128
  172.9 1.9 %multiply_subtract_fusion = f32[4,2,128,128]{3,2,1,0:T(8,128)} fusion(f32[4,2,128,128]{3,2,1,0:T(8,128)S(1)} %copy-done, f32[4,2,128,128]{3,2,1,0:T(8,128)} %all-reduce.5.cloned.1.call-done), kind=kLoop, calls=%fused_computation.169 | loop fusion | flops 262144 | bytes 1572864 | tf_op jit(solution)/shard_map/sub | solution.py:129
  (66 shorter events, 28.7 us)
Async XLA Ops:
  7.2 88.4 %all-reduce.3.cloned.1.call-start = ((), (), s32[]{:S(2)}) async-start(), calls=%async_computation | async-start | bytes 1048576 | tf_op jit(solution)/shard_map/psum | solution.py:128
  7.2 7.9 %collective-permute-start = (f32[2,128,128]{2,1,0:T(8,128)}, f32[2,128,128]{2,1,0:T(8,128)S(1)}, u32[]{:S(2)}, u32[]{:S(2)}) collective-permute-start(f32[2,128,128]{2,1,0:T(8,128)} %param.23), channel_id=1, source_target_pairs={{0,2},{2,4},{4,6},{6,8},{8,10},{10,12},{12,14},{1,3},{3,5},{5,7},{... | collective-permute-start | bytes 393224 | tf_op jit(solution)/shard_map/ppermute | solution.py:17
  12.1 7.1 %collective-permute-start.1 = (f32[2,128,128]{2,1,0:T(8,128)}, f32[2,128,128]{2,1,0:T(8,128)S(1)}, u32[]{:S(2)}, u32[]{:S(2)}) collective-permute-start(f32[2,128,128]{2,1,0:T(8,128)} %param.23), channel_id=1, source_target_pairs={{2,0},{4,2},{6,4},{8,6},{10,8},{12,10},{14,12},{3,1},{5,3},{7,5},{... | collective-permute-start | bytes 393224 | tf_op jit(solution)/shard_map/ppermute | solution.py:20
  19.2 3.7 %collective-permute-start.2 = (f32[2,384,128]{2,1,0:T(8,128)S(1)}, f32[2,384,128]{2,1,0:T(8,128)S(1)}, u32[]{:S(2)}, u32[]{:S(2)}) collective-permute-start(f32[2,384,128]{2,1,0:T(8,128)S(1)} %constant_dynamic-update-slice_fusion), channel_id=1, source_target_pairs={{0,1},{2,3},{4,5},{6,7},{8,9},{10,11},{12,13},{14,15},{16,17},{18,... | collective-permute-start | bytes 1179656 | tf_op jit(solution)/shard_map/ppermute | solution.py:17
  20.5 3.6 %collective-permute-start.3 = (f32[2,384,128]{2,1,0:T(8,128)S(1)}, f32[2,384,128]{2,1,0:T(8,128)S(1)}, u32[]{:S(2)}, u32[]{:S(2)}) collective-permute-start(f32[2,384,128]{2,1,0:T(8,128)S(1)} %constant_dynamic-update-slice_fusion), channel_id=1, source_target_pairs={{1,0},{3,2},{5,4},{7,6},{9,8},{11,10},{13,12},{15,14},{17,16},{19,... | collective-permute-start | bytes 1179656 | tf_op jit(solution)/shard_map/ppermute | solution.py:20
  25.2 0.9 copy-start.1
  25.2 0.9 copy-start.3
  68.2 20.8 %collective-permute-start.4 = (f32[2,128,384]{2,1,0:T(8,128)S(1)}, f32[2,128,384]{2,1,0:T(8,128)S(1)}, u32[]{:S(2)}, u32[]{:S(2)}) collective-permute-start(f32[2,128,384]{2,1,0:T(8,128)S(1)} %get-tuple-element.457), channel_id=1, source_target_pairs={{0,2},{2,4},{4,6},{6,8},{8,10},{10,12},{12,14},{1,3},{3,5},{5,7},{... | collective-permute-start | bytes 1179656 | tf_op jit(solution)/shard_map/ppermute | solution.py:17
  72.8 16.3 %collective-permute-start.5 = (f32[2,128,384]{2,1,0:T(8,128)S(1)}, f32[2,128,384]{2,1,0:T(8,128)S(1)}, u32[]{:S(2)}, u32[]{:S(2)}) collective-permute-start(f32[2,128,384]{2,1,0:T(8,128)S(1)} %get-tuple-element.458), channel_id=1, source_target_pairs={{2,0},{4,2},{6,4},{8,6},{10,8},{12,10},{14,12},{3,1},{5,3},{7,5},{... | collective-permute-start | bytes 1179656 | tf_op jit(solution)/shard_map/ppermute | solution.py:20
  74.9 24.2 %copy-start = (f32[4,2,128,128]{3,2,1,0:T(8,128)S(1)}, f32[4,2,128,128]{3,2,1,0:T(8,128)}, u32[]{:S(2)}) copy-start(f32[4,2,128,128]{3,2,1,0:T(8,128)} %param.24) | copy-start | bytes 1572868
  74.9 98.0 %all-reduce.5.cloned.1.call-start = ((), (), s32[]{:S(2)}) async-start(), calls=%async_computation.1 | async-start | bytes 1048576 | tf_op jit(solution)/shard_map/psum | solution.py:128
  89.1 11.9 %copy-start.2 = (f32[2,128,128]{2,1,0:T(8,128)S(1)}, f32[2,128,128]{2,1,0:T(8,128)}, u32[]{:S(2)}) copy-start(f32[2,128,128]{2,1,0:T(8,128)} %param.23) | copy-start | bytes 393220
  95.6 4.8 %collective-permute-start.6 = (f32[2,128,128]{2,1,0:T(8,128)S(1)}, f32[2,128,128]{2,1,0:T(8,128)S(1)}, u32[]{:S(2)}, u32[]{:S(2)}) collective-permute-start(f32[2,128,128]{2,1,0:T(8,128)S(1)} %get-tuple-element.459), channel_id=1, source_target_pairs={{0,1},{2,3},{4,5},{6,7},{8,9},{10,11},{12,13},{14,15},{16,17},{18,... | collective-permute-start | bytes 393224 | tf_op jit(solution)/shard_map/ppermute | solution.py:17
  97.8 3.2 %collective-permute-start.7 = (f32[2,128,128]{2,1,0:T(8,128)S(1)}, f32[2,128,128]{2,1,0:T(8,128)S(1)}, u32[]{:S(2)}, u32[]{:S(2)}) collective-permute-start(f32[2,128,128]{2,1,0:T(8,128)S(1)} %get-tuple-element.460), channel_id=1, source_target_pairs={{1,0},{3,2},{5,4},{7,6},{9,8},{11,10},{13,12},{15,14},{17,16},{19,... | collective-permute-start | bytes 393224 | tf_op jit(solution)/shard_map/ppermute | solution.py:20
Sparse Core Ops, SparseCore 0:
  75.0 20.4 all-reduce.2
  99.0 73.8 all-reduce.4
